TPU v7x, 32 devices: a whole 2x2x4 slice. The times are simulated.
32 devices in a mesh: gx: 2 (over x), gy: 4 (over z), gz: 4 (over y, core).
Axes of the slice: x: 2, y: 2, z: 4, core: 2. Of those that a mesh axis runs over, the one named last changes fastest.
Arguments:
- state_old: float32 [5, 32, 128, 512], P(None, 'gx', 'gy', 'gz'), as said below
- state_section: float32 [5, 32, 128, 512], P(None, 'gx', 'gy', 'gz'), as said below
- panel_record: bfloat16 [131072, 512], P(('gx', 'gy', 'gz')), may hold values from -6 to 6
- panel_cell: int32 [1024, 128], P(('gx', 'gy', 'gz')), may hold values from 0 to 65535
- panel_angles: float32 [2, 131072], P(None, ('gx', 'gy', 'gz')), may hold values from -3.140625 to 3.140625
- owned_blocks: int32 [32], P(('gx', 'gy', 'gz')), may hold values from 1 to 32, 256 in all
- listener_angles: float32 [2, 1024], replicated, may hold values from -3.140625 to 3.140625
- listener_range: float32 [1024], replicated, may hold values from 1.2 to 2.5
Outputs:
- state_next: float32 [5, 32, 128, 512], P(None, 'gx', 'gy', 'gz')
- observer_spectra: float32 [2, 1024, 128], P(None, 'gz')
Inputs may be any that keep to these rules, and one draw needn't show every extreme that they name: `state_old`: density between 0.5 and 2, velocity components of magnitude 0.3 at most, stiffened-gas pressure between 0.3 and 2. `state_section`: density between 0.5 and 2, velocity components of magnitude 0.3 at most, stiffened-gas pressure between 0.3 and 2. A device's live blocks fill its first owned_blocks slots; some device owns 32 blocks, and they total 8 times the number of devices.
All inputs are finite; a program needn't handle non-finite values.
Results may differ from a plain program's by a relative error of at most 0.0003.
The roundings to bfloat16 on the way count: a program that leaves them out, or rounds other values in their place, can miss the bound.
Values may be sent and summed in bfloat16 or wider, within the bound.
No kernel may reach another device: no remote copies, remote signals or barrier semaphores. Data moves between devices by JAX's collectives and lax.ppermute only.
A program may use at most 64 MiB of HBM per device.

v0:
```python
import math
import jax
import jax.numpy as jnp
from jax import lax
from jax.sharding import PartitionSpec as P

FREQS = 128
GROUP = 4
GAMMA_GAS = 4.4
PRESSURE_INF = 1.0
WENO_EPS = 1e-06
WAVE_STEP = 0.25
COURANT = 0.08


def with_halo(shard, sides, width):
    for axis, dim in sides:
        size, length = (lax.axis_size(axis), shard.shape[dim])
        up = [(i, (i + 1) % size) for i in range(size)]
        down = [(j, i) for i, j in up]
        last = lax.slice_in_dim(shard, length - width, length, axis=dim)
        initial = lax.slice_in_dim(shard, 0, width, axis=dim)
        before = lax.ppermute(last, axis, up)
        after = lax.ppermute(initial, axis, down)
        shard = jnp.concatenate([before, shard, after], axis=dim)
    return shard


def weno_face(far_left, near_left, middle, near_right, far_right):
    cand_a = (2.0 * far_left - 7.0 * near_left + 11.0 * middle) / 6.0
    cand_b = (-near_left + 5.0 * middle + 2.0 * near_right) / 6.0
    cand_c = (2.0 * middle + 5.0 * near_right - far_right) / 6.0
    rough_a = (
        13.0 / 12.0 * (far_left - 2.0 * near_left + middle) ** 2
        + 0.25 * (far_left - 4.0 * near_left + 3.0 * middle) ** 2
    )
    rough_b = (
        13.0 / 12.0 * (near_left - 2.0 * middle + near_right) ** 2
        + 0.25 * (near_left - near_right) ** 2
    )
    rough_c = (
        13.0 / 12.0 * (middle - 2.0 * near_right + far_right) ** 2
        + 0.25 * (3.0 * middle - 4.0 * near_right + far_right) ** 2
    )
    weight_a = 0.1 / (WENO_EPS + rough_a) ** 2
    weight_b = 0.6 / (WENO_EPS + rough_b) ** 2
    weight_c = 0.3 / (WENO_EPS + rough_c) ** 2
    return (weight_a * cand_a + weight_b * cand_b + weight_c * cand_c) / (
        weight_a + weight_b + weight_c
    )


def euler_flux(state_slab, axis_d):
    density = state_slab[0]
    momenta = state_slab[1:4]
    energy = state_slab[4]
    velocity = momenta / density[None]
    kinetic = 0.5 * jnp.sum(momenta * velocity, axis=0)
    pressure = (GAMMA_GAS - 1.0) * (energy - kinetic) - GAMMA_GAS * PRESSURE_INF
    normal_speed = velocity[axis_d]
    sound_speed = jnp.sqrt(GAMMA_GAS * (pressure + PRESSURE_INF) / density)
    rows_out = [momenta[axis_d]]
    for component in range(3):
        carried = momenta[component] * normal_speed
        if component == axis_d:
            carried = carried + pressure
        rows_out.append(carried)
    rows_out.append((energy + pressure) * normal_speed)
    return (jnp.stack(rows_out), jnp.abs(normal_speed) + sound_speed)


def face_difference(padded, axis_d, count_d):
    array_axis = axis_d + 1
    picker = [slice(None), slice(3, -3), slice(3, -3), slice(3, -3)]
    picker[array_axis] = slice(None)
    state_slab = padded[tuple(picker)]
    fluxes, speeds = euler_flux(state_slab, axis_d)
    cell_count = state_slab.shape[array_axis] - 6

    def shifted(values, offset, along):
        return lax.slice_in_dim(values, offset, offset + cell_count + 1, axis=along)

    wave_speed = shifted(speeds, 0, axis_d)
    for offset in range(1, 6):
        wave_speed = jnp.maximum(wave_speed, shifted(speeds, offset, axis_d))
    split_up = [
        0.5
        * (
            shifted(fluxes, offset, array_axis)
            + wave_speed[None] * shifted(state_slab, offset, array_axis)
        )
        for offset in range(6)
    ]
    split_down = [
        0.5
        * (
            shifted(fluxes, offset, array_axis)
            - wave_speed[None] * shifted(state_slab, offset, array_axis)
        )
        for offset in range(6)
    ]
    face_flux = weno_face(
        split_up[0], split_up[1], split_up[2], split_up[3], split_up[4]
    ) + weno_face(split_down[5], split_down[4], split_down[3], split_down[2], split_down[1])
    after = lax.slice_in_dim(face_flux, 1, cell_count + 1, axis=array_axis)
    before = lax.slice_in_dim(face_flux, 0, cell_count, axis=array_axis)
    return (after - before) * float(count_d)


def section_update(padded, old_block, counts, step_size):
    change = (
        face_difference(padded, 0, counts[0])
        + face_difference(padded, 1, counts[1])
        + face_difference(padded, 2, counts[2])
    )
    return 0.75 * old_block + 0.25 * (padded[:, 3:-3, 3:-3, 3:-3] - step_size * change)


def directions(angles):
    polar_angle = 0.5 * angles[0]
    azimuth = angles[1]
    return jnp.stack(
        [
            jnp.cos(polar_angle) * jnp.cos(azimuth),
            jnp.cos(polar_angle) * jnp.sin(azimuth),
            jnp.sin(polar_angle),
        ]
    )


def panel_places(cell_rows, block_x, block_y, block_z, cells_x, cells_y, cells_z, counts):
    along_x = cell_rows // (cells_y * cells_z)
    along_y = cell_rows // cells_z % cells_y
    along_z = cell_rows % cells_z
    place_x = ((block_x * cells_x + along_x).astype(jnp.float32) + 0.5) / counts[0]
    place_y = ((block_y * cells_y + along_y).astype(jnp.float32) + 0.5) / counts[1]
    place_z = ((block_z * cells_z + along_z).astype(jnp.float32) + 0.5) / counts[2]
    return jnp.stack([place_x, place_y, place_z], axis=1)


def dft_table(sample_count, freq_count):
    times = jnp.arange(sample_count, dtype=jnp.int32)[:, None]
    orders = jnp.arange(1, freq_count + 1, dtype=jnp.int32)[None, :]
    phases = 2.0 * math.pi / sample_count * (times * orders % sample_count).astype(jnp.float32)
    scaling = 1.0 / math.sqrt(sample_count)
    return (jnp.concatenate([jnp.cos(phases), -jnp.sin(phases)], axis=1) * scaling).astype(
        jnp.bfloat16
    )


def observer_group(sources, geometry, live_flags, dft_rows, listeners, wave_numbers):
    places = geometry[:, 0:3]
    normals = geometry[:, 3:6]
    spectra = jnp.einsum(
        "gpt,tk->gpk", sources, dft_rows, preferred_element_type=jnp.float32
    ).astype(jnp.bfloat16)
    offsets = listeners[None, :, :, None] - places[:, :, None, :]
    dist_sq = jnp.sum(offsets * offsets, axis=1)
    facing = jnp.sum(normals[:, :, None, :] * offsets, axis=1)
    weights = (facing / (4.0 * math.pi * dist_sq)).astype(jnp.bfloat16)
    product = jnp.einsum("gop,gpk->gok", weights, spectra, preferred_element_type=jnp.float32)
    centres = jnp.mean(places, axis=2)
    separation = listeners[None, :, :] - centres[:, :, None]
    centre_reach = jnp.sqrt(jnp.sum(separation * separation, axis=1))
    phase_now = centre_reach[:, :, None] * wave_numbers[None, None, :]
    cosine = jnp.cos(phase_now)
    sine_part = jnp.sin(phase_now)
    freq_count = wave_numbers.shape[0]
    real_part = product[:, :, :freq_count] * cosine + product[:, :, freq_count:] * sine_part
    imag_part = product[:, :, freq_count:] * cosine - product[:, :, :freq_count] * sine_part
    masks = live_flags[:, None, None]
    return jnp.stack([jnp.sum(masks * real_part, axis=0), jnp.sum(masks * imag_part, axis=0)])


def local(
    state_old,
    state_section,
    panel_record,
    panel_cell,
    panel_angles,
    owned_blocks,
    listener_angles,
    listener_range,
):
    cells_x = state_section.shape[1]
    cells_y = state_section.shape[2]
    cells_z = state_section.shape[3]
    counts = (
        cells_x * lax.axis_size("gx"),
        cells_y * lax.axis_size("gy"),
        cells_z * lax.axis_size("gz"),
    )
    step_size = COURANT / max(counts)
    padded = with_halo(state_section, (("gx", 1), ("gy", 2), ("gz", 3)), 3)
    updated = section_update(padded, state_old, counts, step_size)
    slot_count = panel_cell.shape[0]
    block_rows = panel_cell.shape[1]
    samples = panel_record.shape[1]
    density = updated[0].reshape(cells_x * cells_y * cells_z)
    sampled = density[panel_cell]
    sources = (
        panel_record.reshape(slot_count, block_rows, samples).astype(jnp.float32)
        * sampled[:, :, None]
    ).astype(jnp.bfloat16)
    places = panel_places(
        panel_cell,
        lax.axis_index("gx"),
        lax.axis_index("gy"),
        lax.axis_index("gz"),
        cells_x,
        cells_y,
        cells_z,
        counts,
    )
    normals = jnp.transpose(directions(panel_angles.reshape(2, slot_count, block_rows)), (1, 0, 2))
    geometry = jnp.concatenate([places, normals], axis=1)
    live_count = owned_blocks[0]
    live_flags = (jnp.arange(slot_count, dtype=jnp.int32) < live_count).astype(jnp.float32)
    dft_rows = dft_table(samples, FREQS)
    listeners = 0.5 + listener_range[None, :] * directions(listener_angles)
    wave_numbers = WAVE_STEP * jnp.arange(1, FREQS + 1, dtype=jnp.int32).astype(jnp.float32)

    def add_group(group_turn, running):
        first_row = group_turn * GROUP
        group_sources = lax.dynamic_slice_in_dim(sources, first_row, GROUP, 0)
        group_geometry = lax.dynamic_slice_in_dim(geometry, first_row, GROUP, 0)
        group_flags = lax.dynamic_slice_in_dim(live_flags, first_row, GROUP, 0)
        return running + observer_group(
            group_sources, group_geometry, group_flags, dft_rows, listeners, wave_numbers
        )

    group_total = (live_count + GROUP - 1) // GROUP
    running = lax.fori_loop(
        0, group_total, add_group, jnp.zeros((2, listeners.shape[1], FREQS), jnp.float32)
    )
    gz_share = lax.psum_scatter(running, "gz", scatter_dimension=1, tiled=True)
    spectra_out = lax.psum(gz_share, ("gx", "gy"))
    return (updated, spectra_out)


def solution(mesh):
    return jax.shard_map(
        local,
        mesh=mesh,
        in_specs=(
            P(None, "gx", "gy", "gz"),
            P(None, "gx", "gy", "gz"),
            P(("gx", "gy", "gz"), None),
            P(("gx", "gy", "gz"), None),
            P(None, ("gx", "gy", "gz")),
            P(("gx", "gy", "gz")),
            P(),
            P(),
        ),
        out_specs=(P(None, "gx", "gy", "gz"), P(None, "gz", None)),
        check_vma=False,
    )
```

profile of v0, /device:TPU:0, one launch (start us, length us, event | category | flops | bytes accessed | tf_op | source)
XLA Modules:
  0.0 392.4 jit_solution(911386908631650255)
XLA Ops:
  7.2 1.9 fusion.121
  9.1 3.0 collective-permute-start
  12.8 1.8 multiply_bitcast_fusion.1
  14.6 1.0 cosine_multiply_fusion
  15.6 1.1 fusion.95
  16.6 0.8 fusion.60
  17.5 0.7 pad_maximum_fusion.7
  18.3 0.7 collective-permute-done
  19.0 1.0 constant_dynamic-update-slice_fusion.4
  20.3 3.0 collective-permute-done.1
  24.4 1.9 collective-permute-start.2
  26.3 2.1 collective-permute-start.3
  28.4 7.8 %divide_add_fusion.2 = f32[5,17,32,128]{3,2,1,0:T(8,128)} fusion(f32[5,19,32,128]{3,2,1,0:T(8,128)S(1)} %get-tuple-element.123, f32[5,22,32,128]{3,2,1,0:T(8,128)S(1)} %multiply_dynamic-update-slice_fusion.1, f32[5,19,32,128]{3,2,1,0:T(8,128)S(1)} %get-tuple-element.116, f32[17,32,128]{2,1,0:T(8,128)S(1)} %slice_maximum_fusion.10), kind=kLoop, calls=%fused_computation.92 | loop fusion | flops 51179520 | bytes 18382848 | tf_op jit(solution)/shard_map/add | solution.py:102
  36.2 1.0 collective-permute-done.3
  37.2 0.4 pad_maximum_fusion.2
  37.6 0.3 copy-done.5
  38.0 2.7 fusion.119
  41.1 0.9 slice_maximum_fusion.5
  42.2 3.3 copy.41
  45.5 3.3 copy.42
  48.7 1.7 collective-permute-start.5
  50.5 11.8 %divide_add_fusion.1 = f32[5,16,33,128]{3,2,1,0:T(8,128)} fusion(f32[5,22,3,128]{3,2,1,0:T(4,128)} %copy-done.5, f32[5,22,32,128]{3,2,1,0:T(8,128)S(1)} %get-tuple-element.124, f32[5,16,38,128]{3,2,1,0:T(8,128)S(1)} %multiply_dynamic-update-slice_fusion.2, f32[5,22,3,128]{3,2,1,0:T(4,128)} %copy-done.3, f32[16,33,128]{2,1,0:T(8,128)} %slice_maximum_fusion.5), kind=kLoop, calls=%fused_computation.75 | loop fusion | flops 51701760 | bytes 11872256 | tf_op jit(solution)/shard_map/add | solution.py:102
  62.3 3.2 copy.43
  65.5 3.2 copy.44
  68.7 4.9 %pad_maximum_fusion = f32[5,22,38,134]{3,2,1,0:T(8,128)S(1)} fusion(f32[5,22,38,3]{3,2,1,0:T(8,128)} %copy.44, f32[5,22,3,128]{3,2,1,0:T(4,128)S(1)} %copy-done.6, f32[5,22,32,128]{3,2,1,0:T(8,128)S(1)} %get-tuple-element.124, f32[5,22,3,128]{3,2,1,0:T(4,128)S(1)} %copy-done.4, f32[5,22,38,3]{3,2,1,0:T(8,128)} %copy.43), kind=kLoop, calls=%fused_computation.34 | loop fusion | flops 2240480 | bytes 4480960 | tf_op jit(solution)/shard_map/concatenate | solution.py:25
  73.6 0.5 constant_dynamic-update-slice_fusion.7
  74.2 0.4 multiply_reduce_fusion.1
  74.6 0.5 fusion.66
  75.4 0.3 fusion.58
  76.0 0.7 slice_maximum_fusion
  76.8 2.8 maximum_maximum_fusion
  79.6 15.3 %divide_add_fusion = f32[5,16,32,129]{3,2,1,0:T(8,128)S(1)} fusion(f32[5,22,38,131]{3,2,1,0:T(8,128)S(1)} %get-tuple-element.109, f32[5,16,32,134]{3,2,1,0:T(8,128)S(1)} %multiply_dynamic-update-slice_fusion, f32[5,22,38,131]{3,2,1,0:T(8,128)S(1)} %get-tuple-element.108, f32[16,32,129]{2,1,0:T(8,128)S(1)} %slice_maximum_fusion), kind=kLoop, calls=%fused_computation.49 | loop fusion | flops 48545280 | bytes 17436672 | tf_op jit(solution)/shard_map/add | solution.py:102
  95.0 0.8 fusion.54
  95.8 23.0 %gather_fusion = f32[4096]{0:T(1024)S(1)} fusion(f32[65536]{0:T(1024)S(1)} %bitcast.126, s32[4096]{0:T(1024)S(1)} %fusion.111), kind=kCustom, calls=%fused_computation | custom fusion | bytes 49152 | tf_op jit(solution)/shard_map/gather | solution.py:200
  118.9 4.1 %fusion.23 = bf16[32,128,512]{2,1,0:T(8,128)(2,1)} fusion(bf16[32,128,512]{2,1,0:T(8,128)(2,1)} %bitcast.129, f32[32,128]{1,0:T(8,128)S(1)} %bitcast.133), kind=kLoop, calls=%fused_computation.33 | loop fusion | flops 6291456 | bytes 8404992 | tf_op jit(solution)/shard_map/convert_element_type | solution.py:204
  123.1 40.5 %while.11 = (s32[]{:T(128)}, f32[2,1024,128]{2,1,0:T(8,128)S(1)}, s32[]{:T(128)}, f32[32]{0:T(128)S(1)}, f32[32,6,128]{2,1,0:T(8,128)}, /*index=5*/f32[3,1024]{1...) while((s32[]{:T(128)}, f32[2,1024,128]{2,1,0:T(8,128)S(1)}, ...), condition=%wide.region_10.11_spmd.clone, body=%wide.region_3.10_spmd.clone.sunk | while | flops 417236864 | bytes 21886488 | solution.py:233
  123.3 0.9 fusion.130
  124.2 2.9 fusion.131
  127.1 4.8 %fusion.132 = f32[4,1024,256]{2,1,0:T(8,128)} fusion(f32[4,1024,128]{2,1,0:T(8,128)} %get-tuple-element.195, f32[4,1024,128]{2,1,0:T(8,128)S(1)} %get-tuple-element.196, bf16[32,128,512]{2,1,0:T(8,128)(2,1)} %get-tuple-element.232, s32[]{:T(128)S(6)} %select_n.94, bf16[512,256]{1,0:T(8,128)(2,1)S(1)} %get-tuple-element.233), kind=kOutput, calls=%fused_computation.20.clone.1 | convolution fusion | flops 404357120 | bytes 9175044 | tf_op jit(solution)/shard_map/while/body/gop,gpk->gok/dot_general | solution.py:161
  132.2 11.0 %fusion.133 = (f32[1024,128]{1,0:T(8,128)S(1)}, f32[1024,128]{1,0:T(8,128)S(1)}) fusion(f32[4,1024,256]{2,1,0:T(8,128)} %fusion.132, f32[128]{0:T(128)S(1)} %convert_multiply_fusion.3, f32[4,1024]{1,0:T(4,128)S(1)} %sqrt.30, f32[4]{0:T(128)S(1)} %dynamic_slice.18), kind=kLoop, calls=%fused_computation.14.clone.1 | loop fusion | flops 5505024 | bytes 5259792 | tf_op jit(solution)/shard_map/while/body/reduce_sum | solution.py:172
  143.5 0.9 fusion.130
  144.3 2.9 fusion.131
  147.3 4.8 %fusion.132 = f32[4,1024,256]{2,1,0:T(8,128)} fusion(f32[4,1024,128]{2,1,0:T(8,128)} %get-tuple-element.195, f32[4,1024,128]{2,1,0:T(8,128)S(1)} %get-tuple-element.196, bf16[32,128,512]{2,1,0:T(8,128)(2,1)} %get-tuple-element.232, s32[]{:T(128)S(6)} %select_n.94, bf16[512,256]{1,0:T(8,128)(2,1)S(1)} %get-tuple-element.233), kind=kOutput, calls=%fused_computation.20.clone.1 | convolution fusion | flops 404357120 | bytes 9175044 | tf_op jit(solution)/shard_map/while/body/gop,gpk->gok/dot_general | solution.py:161
  152.4 11.0 %fusion.133 = (f32[1024,128]{1,0:T(8,128)S(1)}, f32[1024,128]{1,0:T(8,128)S(1)}) fusion(f32[4,1024,256]{2,1,0:T(8,128)} %fusion.132, f32[128]{0:T(128)S(1)} %convert_multiply_fusion.3, f32[4,1024]{1,0:T(4,128)S(1)} %sqrt.30, f32[4]{0:T(128)S(1)} %dynamic_slice.18), kind=kLoop, calls=%fused_computation.14.clone.1 | loop fusion | flops 5505024 | bytes 5259792 | tf_op jit(solution)/shard_map/while/body/reduce_sum | solution.py:172
  163.6 1.0 copy-done.2
  164.7 144.8 %reduce-scatter.2.cloned.1.call-done = f32[2,256,128]{2,1,0:T(8,128)} async-done(((f32[2,1024,128]{2,1,0:T(8,128)}), f32[2,256,128]{2,1,0:T(8,128)}) %reduce-scatter.2.cloned.1.call-update) | async-done | bytes 262160 | tf_op jit(solution)/shard_map/reduce_scatter | solution.py:236
  309.5 74.4 %all-reduce.2.cloned.1.call-done = f32[2,256,128]{2,1,0:T(8,128)} async-done(((f32[2,256,128]{2,1,0:T(8,128)}), f32[2,256,128]{2,1,0:T(8,128)}) %all-reduce.2.cloned.1.call-update) | async-done | bytes 262160 | tf_op jit(solution)/shard_map/psum | solution.py:237
  383.9 1.7 copy.75
  (82 shorter events, 4.0 us)
Async XLA Ops:
  7.2 12.8 %copy-start.10 = (f32[5,16,32,128]{3,2,1,0:T(8,128)S(1)}, f32[5,16,32,128]{3,2,1,0:T(8,128)}, u32[]{:S(2)}) copy-start(f32[5,16,32,128]{3,2,1,0:T(8,128)} %param.11) | copy-start | bytes 3932164
  7.2 10.3 %copy-start.14 = (s32[32,128]{1,0:T(8,128)S(1)}, s32[32,128]{1,0:T(8,128)}, u32[]{:S(2)}) copy-start(s32[32,128]{1,0:T(8,128)} %param.13) | copy-start | bytes 49156
  7.2 11.1 %copy-start.15 = (f32[1024]{0:T(1024)S(1)}, f32[1024]{0:T(1024)}, u32[]{:S(2)}) copy-start(f32[1024]{0:T(1024)} %param.17) | copy-start | bytes 12292
  7.2 302.3 %reduce-scatter.2.cloned.1.call-start = ((), (), s32[]{:S(2)}) async-start(), calls=%async_computation.1 | async-start | bytes 1310720 | tf_op jit(solution)/shard_map/reduce_scatter | solution.py:236
  9.1 9.9 %collective-permute-start = (f32[5,3,32,128]{3,2,1,0:T(8,128)S(1)}, f32[5,3,32,128]{3,2,1,0:T(8,128)}, u32[]{:S(2)}, u32[]{:S(2)}) collective-permute-start(f32[5,3,32,128]{3,2,1,0:T(8,128)S(1)} %get-tuple-element.120), channel_id=1, source_target_pairs={{0,16},{16,0},{1,17},{17,1},{2,18},{18,2},{3,19},{19,3},{4,20},{20... | collective-permute-start | bytes 737288 | tf_op jit(solution)/shard_map/ppermute | solution.py:23
  12.1 11.2 %collective-permute-start.1 = (f32[5,3,32,128]{3,2,1,0:T(8,128)}, f32[5,3,32,128]{3,2,1,0:T(8,128)S(1)}, u32[]{:S(2)}, u32[]{:S(2)}) collective-permute-start(f32[5,3,32,128]{3,2,1,0:T(8,128)} %get-tuple-element.119), channel_id=1, source_target_pairs={{16,0},{0,16},{17,1},{1,17},{18,2},{2,18},{19,3},{3,19},{20,4},{4,... | collective-permute-start | bytes 737288 | tf_op jit(solution)/shard_map/ppermute | solution.py:24
  24.4 11.8 %collective-permute-start.2 = (f32[5,22,3,128]{3,2,1,0:T(4,128)S(1)}, f32[5,22,3,128]{3,2,1,0:T(4,128)S(1)}, u32[]{:S(2)}, u32[]{:S(2)}) collective-permute-start(f32[5,22,3,128]{3,2,1,0:T(4,128)S(1)} %get-tuple-element.114), channel_id=1, source_target_pairs={{0,4},{4,8},{8,12},{12,0},{1,5},{5,9},{9,13},{13,1},{2,6},{6,10},{... | collective-permute-start | bytes 506888 | tf_op jit(solution)/shard_map/ppermute | solution.py:23
  26.3 10.9 %collective-permute-start.3 = (f32[5,22,3,128]{3,2,1,0:T(4,128)S(1)}, f32[5,22,3,128]{3,2,1,0:T(4,128)S(1)}, u32[]{:S(2)}, u32[]{:S(2)}) collective-permute-start(f32[5,22,3,128]{3,2,1,0:T(4,128)S(1)} %get-tuple-element.115), channel_id=1, source_target_pairs={{4,0},{8,4},{12,8},{0,12},{5,1},{9,5},{13,9},{1,13},{6,2},{10,6},{... | collective-permute-start | bytes 506888 | tf_op jit(solution)/shard_map/ppermute | solution.py:24
  36.2 1.4 copy-start.3
  37.2 0.7 copy-start.5
  45.5 16.8 %collective-permute-start.4 = (f32[5,22,38,3]{2,1,3,0:T(8,128)}, f32[5,22,38,3]{2,1,3,0:T(8,128)}, u32[]{:S(2)}, u32[]{:S(2)}) collective-permute-start(f32[5,22,38,3]{2,1,3,0:T(8,128)} %copy.41), channel_id=1, source_target_pairs={{0,1},{1,2},{2,3},{3,0},{4,5},{5,6},{6,7},{7,4},{8,9},{9,10},{10,1... | collective-permute-start | bytes 150488 | tf_op jit(solution)/shard_map/ppermute | solution.py:23
  48.7 16.7 %collective-permute-start.5 = (f32[5,22,38,3]{2,1,3,0:T(8,128)}, f32[5,22,38,3]{2,1,3,0:T(8,128)}, u32[]{:S(2)}, u32[]{:S(2)}) collective-permute-start(f32[5,22,38,3]{2,1,3,0:T(8,128)} %copy.42), channel_id=1, source_target_pairs={{1,0},{2,1},{3,2},{0,3},{5,4},{6,5},{7,6},{4,7},{9,8},{10,9},{11,1... | collective-permute-start | bytes 150488 | tf_op jit(solution)/shard_map/ppermute | solution.py:24
  65.5 3.2 copy-start.4
  65.5 3.2 copy-start.6
  68.7 4.9 %copy-start = (f32[5,22,38,3]{3,2,1,0:T(8,128)S(1)}, f32[5,22,38,3]{3,2,1,0:T(8,128)}, u32[]{:S(2)}) copy-start(f32[5,22,38,3]{3,2,1,0:T(8,128)} %copy.43) | copy-start | bytes 150484
  68.7 4.9 %copy-start.1 = (f32[5,22,38,3]{3,2,1,0:T(8,128)S(1)}, f32[5,22,38,3]{3,2,1,0:T(8,128)}, u32[]{:S(2)}) copy-start(f32[5,22,38,3]{3,2,1,0:T(8,128)} %copy.44) | copy-start | bytes 150484
  79.6 15.4 %copy-start.7 = (f32[5,17,32,128]{3,2,1,0:T(8,128)S(1)}, f32[5,17,32,128]{3,2,1,0:T(8,128)}, u32[]{:S(2)}) copy-start(f32[5,17,32,128]{3,2,1,0:T(8,128)} %divide_add_fusion.2) | copy-start | bytes 4177924
  79.6 15.4 %copy-start.8 = (f32[5,16,33,128]{3,2,1,0:T(8,128)S(1)}, f32[5,16,33,128]{3,2,1,0:T(8,128)}, u32[]{:S(2)}) copy-start(f32[5,16,33,128]{3,2,1,0:T(8,128)} %divide_add_fusion.1) | copy-start | bytes 4055044
  79.6 15.4 %copy-start.11 = (f32[5,16,32,128]{3,2,1,0:T(8,128)S(1)}, f32[5,16,32,128]{3,2,1,0:T(8,128)}, u32[]{:S(2)}) copy-start(f32[5,16,32,128]{3,2,1,0:T(8,128)} %param.11) | copy-start | bytes 3932164
  79.6 15.4 %copy-start.13 = (f32[5,16,32,128]{3,2,1,0:T(8,128)S(1)}, f32[5,16,32,128]{3,2,1,0:T(8,128)}, u32[]{:S(2)}) copy-start(f32[5,16,32,128]{3,2,1,0:T(8,128)} %param.10) | copy-start | bytes 3932164
  95.8 23.1 %copy-start.12 = (f32[5,16,32,128]{3,2,1,0:T(8,128)}, f32[5,16,32,128]{3,2,1,0:T(8,128)S(1)}, u32[]{:S(2)}) copy-start(f32[5,16,32,128]{3,2,1,0:T(8,128)S(1)} %fusion.54) | copy-start | bytes 3932164
  118.9 4.2 %copy-start.9 = (bf16[512,256]{1,0:T(8,128)(2,1)S(1)}, bf16[512,256]{1,0:T(8,128)(2,1)}, u32[]{:S(2)}) copy-start(bf16[512,256]{1,0:T(8,128)(2,1)} %fusion.60) | copy-start | bytes 786436
  163.6 1.0 copy-start.2
  164.6 219.2 %all-reduce.2.cloned.1.call-start = ((), (), s32[]{:S(2)}) async-start(), calls=%async_computation.2 | async-start | bytes 524288 | tf_op jit(solution)/shard_map/psum | solution.py:237
Sparse Core Ops, SparseCore 0:
  164.7 144.6 reduce-scatter.1
  312.8 71.0 all-reduce.1
where the time goes:
time: 394 us; the launch traced here: 392 us
  waiting for transfers between devices  224 us (57%)
  other arithmetic  89 us (23%)
  local copies, waits for them, and re-layouts  45.6 us (12%)
  between operations  15.2 us (4%)
  matrix products  9.54 us (2%)
  starting transfers between devices  8.79 us (2%)
    reduce_scatter x1, waiting for transfers between devices, local(): gz_share = lax.psum_scatter(running, 'gz', scatter_dimension=1, tiled=True)  145 us
    psum x1, waiting for transfers between devices, local(): spectra_out = lax.psum(gz_share, ('gx', 'gy'))  74.4 us
    add x3, other arithmetic, face_difference(): weno_face(split_up[0], split_up[1], split_up[2], split_up[3], split_up[4])  34.9 us
    gather x1, local copies, waits for them, and re-layouts, local(): sampled = density[panel_cell]  23 us
    reduce_sum x2, other arithmetic, observer_group(): jnp.sum(masks * real_part, axis=0)  22 us
    dot_general x2, matrix products, observer_group(): jnp.einsum('gop,gpk->gok', weights, spectra, preferred_element_type=jnp.f...  9.54 us
    concatenate x3, other arithmetic, with_halo(): shard = jnp.concatenate([before, shard, after], axis=dim)  8.06 us
  transfers between devices with their start and end apart: 8, of which 5 were waited for; matrix products, arithmetic and copies ran while one was open for 8% of the time, Pallas kernels for 0%

commit v1 on v0

--- a/solution.py
+++ b/solution.py
@@ -234,7 +234,7 @@
         0, group_total, add_group, jnp.zeros((2, listeners.shape[1], FREQS), jnp.float32)
     )
     gz_share = lax.psum_scatter(running, "gz", scatter_dimension=1, tiled=True)
-    spectra_out = lax.psum(gz_share, ("gx", "gy"))
+    spectra_out = jnp.sum(lax.all_gather(gz_share, ("gx", "gy")), axis=0)
     return (updated, spectra_out)
 
 

time: 394 us -> 372 us (0.944)
  waiting for transfers between devices: 224 us -> 201 us
    psum x1 -> x0, waiting for transfers between devices: 74.4 us -> none  [local(): spectra_out = lax.psum(gz_share, ('gx', 'gy'))]
    all_gather x0 -> x1, waiting for transfers between devices: none -> 51.2 us  [local(): spectra_out = jnp.sum(lax.all_gather(gz_share, ('gx', 'gy')), axis=0)]
  transfers between devices with their start and end apart: 8 -> 8, of which waited for: 5 -> 5; matrix products, arithmetic and copies ran while one was open for 8% -> 9% of each run, Pallas kernels for 0% -> 0%
where the time goes in v1:
time: 372 us; the launch traced here: 370 us
  waiting for transfers between devices  201 us (54%)
  other arithmetic  91.4 us (25%)
  local copies, waits for them, and re-layouts  43.9 us (12%)
  between operations  15.2 us (4%)
  matrix products  9.54 us (3%)
  starting transfers between devices  8.79 us (2%)
    reduce_scatter x1, waiting for transfers between devices, local(): gz_share = lax.psum_scatter(running, 'gz', scatter_dimension=1, tiled=True)  145 us
    all_gather x1, waiting for transfers between devices, local(): spectra_out = jnp.sum(lax.all_gather(gz_share, ('gx', 'gy')), axis=0)  51.2 us
    add x3, other arithmetic, face_difference(): weno_face(split_up[0], split_up[1], split_up[2], split_up[3], split_up[4])  34.9 us
    gather x1, local copies, waits for them, and re-layouts, local(): sampled = density[panel_cell]  23 us
    reduce_sum x2, other arithmetic, observer_group(): jnp.sum(masks * real_part, axis=0)  22 us
    dot_general x2, matrix products, observer_group(): jnp.einsum('gop,gpk->gok', weights, spectra, preferred_element_type=jnp.f...  9.54 us
    concatenate x3, other arithmetic, with_halo(): shard = jnp.concatenate([before, shard, after], axis=dim)  8.06 us
  transfers between devices with their start and end apart: 8, of which 5 were waited for; matrix products, arithmetic and copies ran while one was open for 9% of the time, Pallas kernels for 0%

profile of v1, /device:TPU:0, one launch (start us, length us, event | category | flops | bytes accessed | tf_op | source)
XLA Modules:
  0.0 369.9 jit_solution(11389371042494974883)
XLA Ops:
  7.2 1.9 fusion.121
  9.1 3.0 collective-permute-start
  12.8 1.8 multiply_bitcast_fusion.1
  14.6 1.0 cosine_multiply_fusion
  15.6 1.1 fusion.95
  16.6 0.8 fusion.60
  17.5 0.7 pad_maximum_fusion.7
  18.3 0.7 collective-permute-done
  19.0 1.0 constant_dynamic-update-slice_fusion.4
  20.3 3.0 collective-permute-done.1
  24.4 1.9 collective-permute-start.2
  26.3 2.1 collective-permute-start.3
  28.4 7.8 %divide_add_fusion.2 = f32[5,17,32,128]{3,2,1,0:T(8,128)} fusion(f32[5,19,32,128]{3,2,1,0:T(8,128)S(1)} %get-tuple-element.123, f32[5,22,32,128]{3,2,1,0:T(8,128)S(1)} %multiply_dynamic-update-slice_fusion.1, f32[5,19,32,128]{3,2,1,0:T(8,128)S(1)} %get-tuple-element.116, f32[17,32,128]{2,1,0:T(8,128)S(1)} %slice_maximum_fusion.10), kind=kLoop, calls=%fused_computation.92 | loop fusion | flops 51179520 | bytes 18382848 | tf_op jit(solution)/shard_map/add | solution.py:102
  36.2 1.0 collective-permute-done.3
  37.2 0.4 pad_maximum_fusion.2
  37.6 0.3 copy-done.5
  38.0 2.7 fusion.119
  41.1 0.9 slice_maximum_fusion.5
  42.2 3.3 copy.41
  45.5 3.3 copy.42
  48.7 1.7 collective-permute-start.5
  50.5 11.8 %divide_add_fusion.1 = f32[5,16,33,128]{3,2,1,0:T(8,128)} fusion(f32[5,22,3,128]{3,2,1,0:T(4,128)} %copy-done.5, f32[5,22,32,128]{3,2,1,0:T(8,128)S(1)} %get-tuple-element.124, f32[5,16,38,128]{3,2,1,0:T(8,128)S(1)} %multiply_dynamic-update-slice_fusion.2, f32[5,22,3,128]{3,2,1,0:T(4,128)} %copy-done.3, f32[16,33,128]{2,1,0:T(8,128)} %slice_maximum_fusion.5), kind=kLoop, calls=%fused_computation.75 | loop fusion | flops 51701760 | bytes 11872256 | tf_op jit(solution)/shard_map/add | solution.py:102
  62.3 3.2 copy.43
  65.5 3.2 copy.44
  68.7 4.9 %pad_maximum_fusion = f32[5,22,38,134]{3,2,1,0:T(8,128)S(1)} fusion(f32[5,22,38,3]{3,2,1,0:T(8,128)} %copy.44, f32[5,22,3,128]{3,2,1,0:T(4,128)S(1)} %copy-done.6, f32[5,22,32,128]{3,2,1,0:T(8,128)S(1)} %get-tuple-element.124, f32[5,22,3,128]{3,2,1,0:T(4,128)S(1)} %copy-done.4, f32[5,22,38,3]{3,2,1,0:T(8,128)} %copy.43), kind=kLoop, calls=%fused_computation.34 | loop fusion | flops 2240480 | bytes 4480960 | tf_op jit(solution)/shard_map/concatenate | solution.py:25
  73.6 0.5 constant_dynamic-update-slice_fusion.7
  74.2 0.4 multiply_reduce_fusion.1
  74.6 0.5 fusion.66
  75.4 0.3 fusion.58
  76.0 0.7 slice_maximum_fusion
  76.8 2.8 maximum_maximum_fusion
  79.6 15.3 %divide_add_fusion = f32[5,16,32,129]{3,2,1,0:T(8,128)S(1)} fusion(f32[5,22,38,131]{3,2,1,0:T(8,128)S(1)} %get-tuple-element.109, f32[5,16,32,134]{3,2,1,0:T(8,128)S(1)} %multiply_dynamic-update-slice_fusion, f32[5,22,38,131]{3,2,1,0:T(8,128)S(1)} %get-tuple-element.108, f32[16,32,129]{2,1,0:T(8,128)S(1)} %slice_maximum_fusion), kind=kLoop, calls=%fused_computation.49 | loop fusion | flops 48545280 | bytes 17436672 | tf_op jit(solution)/shard_map/add | solution.py:102
  95.0 0.8 fusion.54
  95.8 23.0 %gather_fusion = f32[4096]{0:T(1024)S(1)} fusion(f32[65536]{0:T(1024)S(1)} %bitcast.127, s32[4096]{0:T(1024)S(1)} %fusion.111), kind=kCustom, calls=%fused_computation | custom fusion | bytes 49152 | tf_op jit(solution)/shard_map/gather | solution.py:200
  118.9 4.1 %fusion.23 = bf16[32,128,512]{2,1,0:T(8,128)(2,1)} fusion(bf16[32,128,512]{2,1,0:T(8,128)(2,1)} %bitcast.130, f32[32,128]{1,0:T(8,128)S(1)} %bitcast.135), kind=kLoop, calls=%fused_computation.33 | loop fusion | flops 6291456 | bytes 8404992 | tf_op jit(solution)/shard_map/convert_element_type | solution.py:204
  123.1 40.5 %while.11 = (s32[]{:T(128)}, f32[2,1024,128]{2,1,0:T(8,128)S(1)}, s32[]{:T(128)}, f32[32]{0:T(128)S(1)}, f32[32,6,128]{2,1,0:T(8,128)}, /*index=5*/f32[3,1024]{1...) while((s32[]{:T(128)}, f32[2,1024,128]{2,1,0:T(8,128)S(1)}, ...), condition=%wide.region_10.11_spmd.clone, body=%wide.region_3.10_spmd.clone.sunk | while | flops 417236864 | bytes 21886488 | solution.py:233
  123.3 0.9 fusion.130
  124.2 2.9 fusion.131
  127.1 4.8 %fusion.132 = f32[4,1024,256]{2,1,0:T(8,128)} fusion(f32[4,1024,128]{2,1,0:T(8,128)} %get-tuple-element.195, f32[4,1024,128]{2,1,0:T(8,128)S(1)} %get-tuple-element.196, bf16[32,128,512]{2,1,0:T(8,128)(2,1)} %get-tuple-element.232, s32[]{:T(128)S(6)} %select_n.94, bf16[512,256]{1,0:T(8,128)(2,1)S(1)} %get-tuple-element.233), kind=kOutput, calls=%fused_computation.20.clone.1 | convolution fusion | flops 404357120 | bytes 9175044 | tf_op jit(solution)/shard_map/while/body/gop,gpk->gok/dot_general | solution.py:161
  132.2 11.0 %fusion.133 = (f32[1024,128]{1,0:T(8,128)S(1)}, f32[1024,128]{1,0:T(8,128)S(1)}) fusion(f32[4,1024,256]{2,1,0:T(8,128)} %fusion.132, f32[128]{0:T(128)S(1)} %convert_multiply_fusion.3, f32[4,1024]{1,0:T(4,128)S(1)} %sqrt.30, f32[4]{0:T(128)S(1)} %dynamic_slice.18), kind=kLoop, calls=%fused_computation.14.clone.1 | loop fusion | flops 5505024 | bytes 5259792 | tf_op jit(solution)/shard_map/while/body/reduce_sum | solution.py:172
  143.5 0.9 fusion.130
  144.3 2.9 fusion.131
  147.3 4.8 %fusion.132 = f32[4,1024,256]{2,1,0:T(8,128)} fusion(f32[4,1024,128]{2,1,0:T(8,128)} %get-tuple-element.195, f32[4,1024,128]{2,1,0:T(8,128)S(1)} %get-tuple-element.196, bf16[32,128,512]{2,1,0:T(8,128)(2,1)} %get-tuple-element.232, s32[]{:T(128)S(6)} %select_n.94, bf16[512,256]{1,0:T(8,128)(2,1)S(1)} %get-tuple-element.233), kind=kOutput, calls=%fused_computation.20.clone.1 | convolution fusion | flops 404357120 | bytes 9175044 | tf_op jit(solution)/shard_map/while/body/gop,gpk->gok/dot_general | solution.py:161
  152.4 11.0 %fusion.133 = (f32[1024,128]{1,0:T(8,128)S(1)}, f32[1024,128]{1,0:T(8,128)S(1)}) fusion(f32[4,1024,256]{2,1,0:T(8,128)} %fusion.132, f32[128]{0:T(128)S(1)} %convert_multiply_fusion.3, f32[4,1024]{1,0:T(4,128)S(1)} %sqrt.30, f32[4]{0:T(128)S(1)} %dynamic_slice.18), kind=kLoop, calls=%fused_computation.14.clone.1 | loop fusion | flops 5505024 | bytes 5259792 | tf_op jit(solution)/shard_map/while/body/reduce_sum | solution.py:172
  163.6 1.0 copy-done.2
  164.7 144.8 %reduce-scatter.2.cloned.1.call-done = f32[2,256,128]{2,1,0:T(8,128)} async-done(((f32[2,1024,128]{2,1,0:T(8,128)}), f32[2,256,128]{2,1,0:T(8,128)}) %reduce-scatter.2.cloned.1.call-update) | async-done | bytes 262160 | tf_op jit(solution)/shard_map/reduce_scatter | solution.py:236
  309.5 51.2 %all-gather.3.cloned.1.call-done = f32[16,256,128]{2,1,0:T(8,128)} async-done(((f32[2,256,128]{2,1,0:T(8,128)}), f32[16,256,128]{2,1,0:T(8,128)}) %all-gather.3.cloned.1.call-update) | async-done | bytes 2097168 | tf_op jit(solution)/shard_map/all_gather | solution.py:237
  360.7 2.4 reduce_sum.93
  (82 shorter events, 4.0 us)
Async XLA Ops:
  7.2 12.8 %copy-start.10 = (f32[5,16,32,128]{3,2,1,0:T(8,128)S(1)}, f32[5,16,32,128]{3,2,1,0:T(8,128)}, u32[]{:S(2)}) copy-start(f32[5,16,32,128]{3,2,1,0:T(8,128)} %param.11) | copy-start | bytes 3932164
  7.2 10.3 %copy-start.14 = (s32[32,128]{1,0:T(8,128)S(1)}, s32[32,128]{1,0:T(8,128)}, u32[]{:S(2)}) copy-start(s32[32,128]{1,0:T(8,128)} %param.13) | copy-start | bytes 49156
  7.2 11.1 %copy-start.15 = (f32[1024]{0:T(1024)S(1)}, f32[1024]{0:T(1024)}, u32[]{:S(2)}) copy-start(f32[1024]{0:T(1024)} %param.17) | copy-start | bytes 12292
  7.2 302.3 %reduce-scatter.2.cloned.1.call-start = ((), (), s32[]{:S(2)}) async-start(), calls=%async_computation.1 | async-start | bytes 1310720 | tf_op jit(solution)/shard_map/reduce_scatter | solution.py:236
  9.1 9.9 %collective-permute-start = (f32[5,3,32,128]{3,2,1,0:T(8,128)S(1)}, f32[5,3,32,128]{3,2,1,0:T(8,128)}, u32[]{:S(2)}, u32[]{:S(2)}) collective-permute-start(f32[5,3,32,128]{3,2,1,0:T(8,128)S(1)} %get-tuple-element.120), channel_id=1, source_target_pairs={{0,16},{16,0},{1,17},{17,1},{2,18},{18,2},{3,19},{19,3},{4,20},{20... | collective-permute-start | bytes 737288 | tf_op jit(solution)/shard_map/ppermute | solution.py:23
  12.1 11.2 %collective-permute-start.1 = (f32[5,3,32,128]{3,2,1,0:T(8,128)}, f32[5,3,32,128]{3,2,1,0:T(8,128)S(1)}, u32[]{:S(2)}, u32[]{:S(2)}) collective-permute-start(f32[5,3,32,128]{3,2,1,0:T(8,128)} %get-tuple-element.119), channel_id=1, source_target_pairs={{16,0},{0,16},{17,1},{1,17},{18,2},{2,18},{19,3},{3,19},{20,4},{4,... | collective-permute-start | bytes 737288 | tf_op jit(solution)/shard_map/ppermute | solution.py:24
  24.4 11.8 %collective-permute-start.2 = (f32[5,22,3,128]{3,2,1,0:T(4,128)S(1)}, f32[5,22,3,128]{3,2,1,0:T(4,128)S(1)}, u32[]{:S(2)}, u32[]{:S(2)}) collective-permute-start(f32[5,22,3,128]{3,2,1,0:T(4,128)S(1)} %get-tuple-element.114), channel_id=1, source_target_pairs={{0,4},{4,8},{8,12},{12,0},{1,5},{5,9},{9,13},{13,1},{2,6},{6,10},{... | collective-permute-start | bytes 506888 | tf_op jit(solution)/shard_map/ppermute | solution.py:23
  26.3 10.9 %collective-permute-start.3 = (f32[5,22,3,128]{3,2,1,0:T(4,128)S(1)}, f32[5,22,3,128]{3,2,1,0:T(4,128)S(1)}, u32[]{:S(2)}, u32[]{:S(2)}) collective-permute-start(f32[5,22,3,128]{3,2,1,0:T(4,128)S(1)} %get-tuple-element.115), channel_id=1, source_target_pairs={{4,0},{8,4},{12,8},{0,12},{5,1},{9,5},{13,9},{1,13},{6,2},{10,6},{... | collective-permute-start | bytes 506888 | tf_op jit(solution)/shard_map/ppermute | solution.py:24
  36.2 1.4 copy-start.3
  37.2 0.7 copy-start.5
  45.5 16.8 %collective-permute-start.4 = (f32[5,22,38,3]{2,1,3,0:T(8,128)}, f32[5,22,38,3]{2,1,3,0:T(8,128)}, u32[]{:S(2)}, u32[]{:S(2)}) collective-permute-start(f32[5,22,38,3]{2,1,3,0:T(8,128)} %copy.41), channel_id=1, source_target_pairs={{0,1},{1,2},{2,3},{3,0},{4,5},{5,6},{6,7},{7,4},{8,9},{9,10},{10,1... | collective-permute-start | bytes 150488 | tf_op jit(solution)/shard_map/ppermute | solution.py:23
  48.7 16.7 %collective-permute-start.5 = (f32[5,22,38,3]{2,1,3,0:T(8,128)}, f32[5,22,38,3]{2,1,3,0:T(8,128)}, u32[]{:S(2)}, u32[]{:S(2)}) collective-permute-start(f32[5,22,38,3]{2,1,3,0:T(8,128)} %copy.42), channel_id=1, source_target_pairs={{1,0},{2,1},{3,2},{0,3},{5,4},{6,5},{7,6},{4,7},{9,8},{10,9},{11,1... | collective-permute-start | bytes 150488 | tf_op jit(solution)/shard_map/ppermute | solution.py:24
  65.5 3.2 copy-start.4
  65.5 3.2 copy-start.6
  68.7 4.9 %copy-start = (f32[5,22,38,3]{3,2,1,0:T(8,128)S(1)}, f32[5,22,38,3]{3,2,1,0:T(8,128)}, u32[]{:S(2)}) copy-start(f32[5,22,38,3]{3,2,1,0:T(8,128)} %copy.43) | copy-start | bytes 150484
  68.7 4.9 %copy-start.1 = (f32[5,22,38,3]{3,2,1,0:T(8,128)S(1)}, f32[5,22,38,3]{3,2,1,0:T(8,128)}, u32[]{:S(2)}) copy-start(f32[5,22,38,3]{3,2,1,0:T(8,128)} %copy.44) | copy-start | bytes 150484
  79.6 15.4 %copy-start.7 = (f32[5,17,32,128]{3,2,1,0:T(8,128)S(1)}, f32[5,17,32,128]{3,2,1,0:T(8,128)}, u32[]{:S(2)}) copy-start(f32[5,17,32,128]{3,2,1,0:T(8,128)} %divide_add_fusion.2) | copy-start | bytes 4177924
  79.6 15.4 %copy-start.8 = (f32[5,16,33,128]{3,2,1,0:T(8,128)S(1)}, f32[5,16,33,128]{3,2,1,0:T(8,128)}, u32[]{:S(2)}) copy-start(f32[5,16,33,128]{3,2,1,0:T(8,128)} %divide_add_fusion.1) | copy-start | bytes 4055044
  79.6 15.4 %copy-start.11 = (f32[5,16,32,128]{3,2,1,0:T(8,128)S(1)}, f32[5,16,32,128]{3,2,1,0:T(8,128)}, u32[]{:S(2)}) copy-start(f32[5,16,32,128]{3,2,1,0:T(8,128)} %param.11) | copy-start | bytes 3932164
  79.6 15.4 %copy-start.13 = (f32[5,16,32,128]{3,2,1,0:T(8,128)S(1)}, f32[5,16,32,128]{3,2,1,0:T(8,128)}, u32[]{:S(2)}) copy-start(f32[5,16,32,128]{3,2,1,0:T(8,128)} %param.10) | copy-start | bytes 3932164
  95.8 23.1 %copy-start.12 = (f32[5,16,32,128]{3,2,1,0:T(8,128)}, f32[5,16,32,128]{3,2,1,0:T(8,128)S(1)}, u32[]{:S(2)}) copy-start(f32[5,16,32,128]{3,2,1,0:T(8,128)S(1)} %fusion.54) | copy-start | bytes 3932164
  118.9 4.2 %copy-start.9 = (bf16[512,256]{1,0:T(8,128)(2,1)S(1)}, bf16[512,256]{1,0:T(8,128)(2,1)}, u32[]{:S(2)}) copy-start(bf16[512,256]{1,0:T(8,128)(2,1)} %fusion.60) | copy-start | bytes 786436
  163.6 1.0 copy-start.2
  164.6 196.1 %all-gather.3.cloned.1.call-start = ((), (), s32[]{:S(2)}) async-start(), calls=%async_computation.2 | async-start | bytes 2359296 | tf_op jit(solution)/shard_map/all_gather | solution.py:237
Sparse Core Ops, SparseCore 0:
  164.7 144.6 reduce-scatter.1
  311.6 49.0 all-gather.2
